TPU v7x, 32 devices: a whole 2x2x4 slice. The times are simulated.
32 devices in a mesh: section: 4 (over x, core), head: 8 (over z, y).
Axes of the slice: x: 2, y: 2, z: 4, core: 2. Of those that a mesh axis runs over, the one named last changes fastest.
Arguments:
- hidden: float32 [4, 32, 7168], P(None, 'section'), may hold values from -6 to 6
- norm_gain: float32 [7168], replicated, may hold values from 0.5 to 1.5
- router: bfloat16 [7168, 8], replicated, may hold values from -0.0625 to 0.0625
- key_value_weight: bfloat16 [7168, 256], replicated, may hold values from -0.0625 to 0.0625
- query_master: float32 [7168, 1024], P('section', 'head'), may hold values from -0.0625 to 0.0625
- output_master: float32 [7168, 1024], P('section', 'head'), may hold values from -1 to 1
- key_value_cache: bfloat16 [32, 256, 256], P('section', 'head'), may hold values from -480 to 480
- lengths: int32 [32], P('section'), may hold values from 64 to 256
- routes: int32 [4, 32, 4], P(None, 'section'), may hold values from 0 to 7, all different within a row
Outputs:
- handed_on: float32 [4, 32, 7168], P(None, 'section', 'head')
All inputs are finite; a program needn't handle non-finite values.
Results may differ from a plain program's by a relative error of at most 0.012.
The roundings to bfloat16 on the way count: a program that leaves them out, or rounds other values in their place, can miss the bound.
Values may be sent and summed in bfloat16 or wider, within the bound.
No kernel may reach another device: no remote copies, remote signals or barrier semaphores. Data moves between devices by JAX's collectives and lax.ppermute only.
A program may use at most 64 MiB of HBM per device.

v0:
```python
import math

import jax
import jax.numpy as jnp
from jax import lax
from jax.sharding import PartitionSpec as P


def from_behind(value, axis, steps):
    count = lax.axis_size(axis)
    pairs = [(source, (source + steps) % count) for source in range(count)]
    return lax.ppermute(value, axis, pairs)


def body(
    hidden,
    norm_gain,
    router,
    key_value_weight,
    query_master,
    output_master,
    key_value_cache,
    lengths,
    routes,
):
    step_count, row_count, model_width = hidden.shape
    head_dim = key_value_weight.shape[1] // 2
    experts = router.shape[1]
    own_expert = lax.axis_index("head")
    query_piece = query_master.astype(jnp.bfloat16)
    output_piece = output_master.astype(jnp.bfloat16)
    query_weight, output_weight = (
        lax.all_gather(query_piece, "section", axis=0, tiled=True),
        lax.all_gather(output_piece, "section", axis=0, tiled=True),
    )
    mean_square = jnp.mean(hidden * hidden, axis=-1, keepdims=True)
    normed = (hidden * lax.rsqrt(mean_square + 1e-05) * norm_gain).astype(jnp.bfloat16)
    flat_rows = normed.reshape(step_count * row_count, model_width)
    logits = jnp.dot(flat_rows, router, preferred_element_type=jnp.float32).reshape(
        step_count, row_count, experts
    )
    expert_ids = jnp.arange(experts)
    chosen = jnp.sum((routes[..., None] == expert_ids).astype(jnp.float32), axis=2)
    picked = jax.nn.sigmoid(logits) * chosen
    gate_values = picked / jnp.sum(picked, axis=-1, keepdims=True)
    fresh_pairs = jnp.dot(flat_rows, key_value_weight, preferred_element_type=jnp.float32).astype(
        jnp.bfloat16
    )
    fresh_pairs = fresh_pairs.reshape(step_count, row_count, 2 * head_dim)
    key_new = fresh_pairs[..., :head_dim]
    value_new = fresh_pairs[..., head_dim:]
    queries = jnp.dot(flat_rows, query_weight, preferred_element_type=jnp.float32).astype(
        jnp.bfloat16
    )
    queries = queries.reshape(step_count, row_count, head_dim)
    score_factor = 1.0 / math.sqrt(head_dim)
    step_order = jnp.arange(step_count)
    fresh_mask = (step_order[None, :] <= step_order[:, None])[:, None, :]
    fresh_scores = (
        jnp.einsum("srh,urh->sru", queries, key_new, preferred_element_type=jnp.float32)
        * score_factor
    )
    fresh_peak = jnp.max(jnp.where(fresh_mask, fresh_scores, -jnp.inf), axis=-1)
    gathered = lax.all_gather(key_value_cache, "head", axis=1, tiled=True)
    positions = jnp.arange(gathered.shape[1])
    cache_mask = (positions[None, :] < lengths[:, None])[None, :, :]
    cache_scores = (
        jnp.einsum(
            "srh,rph->srp", queries, gathered[..., :head_dim], preferred_element_type=jnp.float32
        )
        * score_factor
    )
    highest = jnp.maximum(
        jnp.max(jnp.where(cache_mask, cache_scores, -jnp.inf), axis=-1), fresh_peak
    )
    cache_weights = jnp.where(cache_mask, jnp.exp(cache_scores - highest[..., None]), 0.0)
    mixture = jnp.einsum(
        "srp,rph->srh", cache_weights, gathered[..., head_dim:], preferred_element_type=jnp.float32
    )
    denominator = jnp.sum(cache_weights, axis=-1)
    fresh_weights = jnp.where(fresh_mask, jnp.exp(fresh_scores - highest[..., None]), 0.0)
    mixture = mixture + jnp.einsum(
        "sru,urh->srh", fresh_weights, value_new, preferred_element_type=jnp.float32
    )
    denominator = denominator + jnp.sum(fresh_weights, axis=-1)
    attended = (mixture / denominator[..., None]).astype(jnp.bfloat16)
    share_width = model_width // lax.axis_size("head")
    feature_slice = lax.all_to_all(output_weight, "head", split_axis=0, concat_axis=1, tiled=True)
    feature_slice = feature_slice.reshape(share_width, experts, head_dim)
    all_attended = lax.all_gather(attended[:, :, None, :], "head", axis=2, tiled=True)
    all_attended = all_attended.reshape(step_count * row_count, experts, head_dim)
    per_expert = jnp.einsum(
        "neh,feh->nef", all_attended, feature_slice, preferred_element_type=jnp.float32
    )
    gates_flat = gate_values.reshape(step_count * row_count, experts)
    summed = jnp.sum(gates_flat[..., None] * per_expert, axis=1)
    summed = summed.reshape(step_count, row_count, share_width)
    own_columns = lax.dynamic_slice_in_dim(hidden, own_expert * share_width, share_width, 2)
    result = own_columns + summed
    return from_behind(result, "section", 1)


def solution(mesh):
    return jax.shard_map(
        body,
        mesh=mesh,
        in_specs=(
            P(None, "section", None),
            P(),
            P(),
            P(),
            P("section", "head"),
            P("section", "head"),
            P("section", "head", None),
            P("section"),
            P(None, "section", None),
        ),
        out_specs=P(None, "section", "head"),
        check_vma=False,
    )
```

profile of v0, /device:TPU:0, one launch (start us, length us, event | category | flops | bytes accessed | tf_op | source)
XLA Modules:
  0.0 139.1 jit_solution(11316484669414816470)
XLA Ops:
  6.5 0.0 copy-start
  6.5 0.0 copy-start.2
  6.5 0.0 copy-start.1
  6.5 0.0 all-gather.9.cloned.1.call-start
  6.5 2.1 %convert_element_type.27 = bf16[1792,128]{1,0:T(8,128)(2,1)} convert(f32[1792,128]{1,0:T(8,128)} %param.14) | non-fusion elementwise | flops 229376 | bytes 1376256 | tf_op jit(solution)/shard_map/convert_element_type | solution.py:31
  8.7 0.0 all-gather.9.cloned.1.call-update
  8.7 0.0 all-gather.5.cloned.1.call-start
  8.8 0.0 copy-done.2
  8.8 0.8 convert_element_type.23
  9.6 0.0 all-gather.5.cloned.1.call-update
  9.6 0.0 all-gather.7.cloned.1.call-start
  9.7 0.7 all-gather.7.cloned.1.call-update
  10.3 0.0 copy-done.1
  10.4 0.2 multiply_reduce_fusion
  10.5 22.2 %all-gather.9.cloned.1.call-done = bf16[7168,128]{1,0:T(8,128)(2,1)} async-done(((bf16[1792,128]{1,0:T(8,128)(2,1)}), bf16[7168,128]{1,0:T(8,128)(2,1)}) %all-gather.9.cloned.1.call-update) | async-done | bytes 1835024 | tf_op jit(solution)/shard_map/all_gather | solution.py:34
  32.7 0.0 copy-start.3
  32.8 0.0 copy-start.4
  32.8 5.6 %all-to-all-start = ((bf16[8,896,128]{2,1,0:T(8,128)(2,1)}), bf16[8,896,128]{2,1,0:T(8,128)(2,1)S(1)}, u32[]{:S(2)}, u32[]{:S(2)}) async-start(bf16[8,896,128]{2,1,0:T(8,128)(2,1)} %bitcast.56), calls=%async_computation | async-start | bytes 3670016 | tf_op jit(solution)/shard_map/all_to_all | solution.py:88
  38.4 0.0 copy-done.3
  38.4 0.0 copy-start.5
  38.4 0.2 multiply_convert_fusion
  38.6 0.0 copy-done.4
  38.6 0.1 convert_reduce_fusion
  38.7 0.1 copy.25
  38.8 0.0 copy-done
  38.8 1.1 fusion.43
  39.9 0.1 mul.60
  40.0 0.0 copy-done.5
  40.0 0.1 iota_compare_fusion.1
  40.1 3.0 %fusion.12 = bf16[4,8,256]{2,1,0:T(8,128)(2,1)S(1)} fusion(bf16[7168,256]{1,0:T(8,128)(2,1)} %param.12, bf16[4,8,7168]{2,1,0:T(8,128)(2,1)S(1)} %multiply_convert_fusion), kind=kOutput, calls=%fused_computation.8 | convolution fusion | flops 117448704 | bytes 4145152 | tf_op jit(solution)/shard_map/dot_general | solution.py:46
  43.1 12.3 %all-gather.5.cloned.1.call-done = bf16[7168,128]{1,0:T(8,128)(2,1)} async-done(((bf16[1792,128]{1,0:T(8,128)(2,1)}), bf16[7168,128]{1,0:T(8,128)(2,1)}) %all-gather.5.cloned.1.call-update) | async-done | bytes 1835024 | tf_op jit(solution)/shard_map/all_gather | solution.py:33
  55.4 1.9 %fusion.21 = bf16[4,8,128]{2,1,0:T(8,128)(2,1)S(1)} fusion(bf16[7168,128]{1,0:T(8,128)(2,1)} %all-gather.5.cloned.1.call-done, bf16[4,8,7168]{2,1,0:T(8,128)(2,1)S(1)} %multiply_convert_fusion), kind=kOutput, calls=%fused_computation.22 | convolution fusion | flops 58724352 | bytes 2301952 | tf_op jit(solution)/shard_map/dot_general | solution.py:52
  57.3 0.1 select_reduce_fusion.1
  57.5 47.6 %all-gather.7.cloned.1.call-done = bf16[8,256,256]{2,1,0:T(8,128)(2,1)} async-done(((bf16[8,32,256]{2,1,0:T(8,128)(2,1)}), bf16[8,256,256]{2,1,0:T(8,128)(2,1)}) %all-gather.7.cloned.1.call-update) | async-done | bytes 1048592 | tf_op jit(solution)/shard_map/all_gather | solution.py:64
  105.1 1.4 select_reduce_fusion
  106.5 0.2 fusion.28
  106.7 1.3 convolution_bitcast_fusion.1
  108.0 0.2 fusion.20
  108.2 18.6 %all-gather = bf16[4,8,1024]{2,0,1:T(4,128)(2,1)S(1)} all-gather(bf16[4,8,128]{2,0,1:T(4,128)(2,1)S(1)} %fusion.20), channel_id=2, replica_groups=mesh['section'=4,'head'=8] {'head'}, dimensions={2}, use_global_device_ids=true | all-gather | bytes 73728 | tf_op jit(solution)/shard_map/all_gather | solution.py:90
  126.9 0.0 all-to-all-done
  126.9 0.7 fusion.8
  127.6 0.1 collective-permute-start
  127.7 4.2 %collective-permute-done = f32[4,8,896]{2,1,0:T(8,128)S(1)} collective-permute-done((f32[4,8,896]{2,1,0:T(8,128)S(1)}, f32[4,8,896]{2,1,0:T(8,128)S(1)}, u32[]{:S(2)}, u32[]{:S(2)}) %collective-permute-start) | collective-permute-done | bytes 114720 | tf_op jit(solution)/shard_map/ppermute | solution.py:12
  131.9 0.6 copy.57
  (11 shorter events, 0.1 us)
Async XLA Ops:
  6.5 32.2 %copy-start = (bf16[7168,8]{0,1:T(8,128)(2,1)S(1)}, bf16[7168,8]{0,1:T(8,128)(2,1)}, u32[]{:S(2)}) copy-start(bf16[7168,8]{0,1:T(8,128)(2,1)} %param.11) | copy-start | bytes 344068
  6.5 2.2 %copy-start.2 = (f32[1792,128]{1,0:T(8,128)S(1)}, f32[1792,128]{1,0:T(8,128)}, u32[]{:S(2)}) copy-start(f32[1792,128]{1,0:T(8,128)} %param.13) | copy-start | bytes 2752516
  6.5 3.8 %copy-start.1 = (f32[4,8,7168]{2,1,0:T(8,128)S(1)}, f32[4,8,7168]{2,1,0:T(8,128)}, u32[]{:S(2)}) copy-start(f32[4,8,7168]{2,1,0:T(8,128)} %param.9) | copy-start | bytes 2752516
  6.5 26.2 %all-gather.9.cloned.1.call-start = ((), (), s32[]{:S(2)}) async-start(), calls=%async_computation.3 | async-start | bytes 2293760 | tf_op jit(solution)/shard_map/all_gather | solution.py:34
  8.7 46.7 %all-gather.5.cloned.1.call-start = ((), (), s32[]{:S(2)}) async-start(), calls=%async_computation.1 | async-start | bytes 2293760 | tf_op jit(solution)/shard_map/all_gather | solution.py:33
  9.6 95.5 %all-gather.7.cloned.1.call-start = ((), (), s32[]{:S(2)}) async-start(), calls=%async_computation.2 | async-start | bytes 1179648 | tf_op jit(solution)/shard_map/all_gather | solution.py:64
  32.7 5.7 %copy-start.3 = (f32[7168]{0:T(1024)S(1)}, f32[7168]{0:T(1024)}, u32[]{:S(2)}) copy-start(f32[7168]{0:T(1024)} %param.10) | copy-start | bytes 86020
  32.8 5.8 %copy-start.4 = (s32[4,8,4]{1,2,0:T(4,128)S(1)}, s32[4,8,4]{1,2,0:T(4,128)}, u32[]{:S(2)}) copy-start(s32[4,8,4]{1,2,0:T(4,128)} %param.17) | copy-start | bytes 1540
  32.8 94.1 %all-to-all-start = ((bf16[8,896,128]{2,1,0:T(8,128)(2,1)}), bf16[8,896,128]{2,1,0:T(8,128)(2,1)S(1)}, u32[]{:S(2)}, u32[]{:S(2)}) async-start(bf16[8,896,128]{2,1,0:T(8,128)(2,1)} %bitcast.56), calls=%async_computation | async-start | bytes 3670016 | tf_op jit(solution)/shard_map/all_to_all | solution.py:88
  38.4 1.6 %copy-start.5 = (s32[8]{0:T(128)S(1)}, s32[8]{0:T(128)}, u32[]{:S(2)}) copy-start(s32[8]{0:T(128)} %param.16) | copy-start | bytes 100
  127.6 4.3 %collective-permute-start = (f32[4,8,896]{2,1,0:T(8,128)S(1)}, f32[4,8,896]{2,1,0:T(8,128)S(1)}, u32[]{:S(2)}, u32[]{:S(2)}) collective-permute-start(f32[4,8,896]{2,1,0:T(8,128)S(1)} %bitcast_add_fusion), channel_id=1, source_target_pairs={{0,8},{8,16},{16,24},{24,0},{1,9},{9,17},{17,25},{25,1},{2,10},{10... | collective-permute-start | bytes 344072 | tf_op jit(solution)/shard_map/ppermute | solution.py:12
Sparse Core Ops, SparseCore 0:
  8.9 23.8 all-gather.8
  34.3 21.0 all-gather.4
  57.6 47.4 all-gather.6
where the time goes:
time: 140 us; the launch traced here: 139 us
  waiting for transfers between devices  87.1 us (62%)
  blocking collectives  18.6 us (13%)
  between operations  13.3 us (10%)
  matrix products  9.74 us (7%)
  starting transfers between devices  5.79 us (4%)
  other arithmetic  3.71 us (3%)
    all_gather x1, waiting for transfers between devices, body(): gathered = lax.all_gather(key_value_cache, 'head', axis=1, tiled=True)  47.6 us
    all_gather x1, waiting for transfers between devices, body(): lax.all_gather(output_piece, 'section', axis=0, tiled=True)  22.2 us
    all_gather x1, blocking collectives, body(): lax.all_gather(attended[:, :, None, :], 'head', axis=2, tiled=True)  18.6 us
    all_gather x1, waiting for transfers between devices, body(): lax.all_gather(query_piece, 'section', axis=0, tiled=True)  12.3 us
    all_to_all x1, starting transfers between devices, body(): lax.all_to_all(output_weight, 'head', split_axis=0, concat_axis=1, tiled=...  5.65 us
    ppermute x1, waiting for transfers between devices, from_behind(): return lax.ppermute(value, axis, pairs)  4.2 us
    dot_general x1, matrix products, body(): jnp.dot(flat_rows, key_value_weight, preferred_element_type=jnp.float32)  2.97 us
  transfers between devices with their start and end apart: 5, of which 4 were waited for; matrix products, arithmetic and copies ran while one was open for 8% of the time, Pallas kernels for 0%

commit v1 on v0

v1 whole, which is shorter than its diff:
```python
import math

import jax
import jax.numpy as jnp
from jax import lax
from jax.sharding import PartitionSpec as P


def shift_pairs(count, offset, stride=1, size=None):
    size = count // stride if size is None else size
    if size & (size - 1) == 0:
        return [(i, i ^ (offset * stride)) for i in range(count)]
    pairs = []
    for i in range(count):
        digit = i // stride % size
        pairs.append((i, i + ((offset - digit) % size - digit) * stride))
    return pairs


def partner(digit, offset, size):
    return digit ^ offset if size & (size - 1) == 0 else (offset - digit) % size


def swap(pick, axis, stride, size):
    count = lax.axis_size(axis)
    digit = lax.axis_index(axis) // stride % size
    offsets = range(1, size) if size & (size - 1) == 0 else range(size)
    arrived = [(digit, pick(digit))] if size & (size - 1) == 0 else []
    for offset in offsets:
        other = partner(digit, offset, size)
        block = lax.ppermute(pick(other), axis, shift_pairs(count, offset, stride, size))
        arrived.append((other, block))
    return arrived


def in_order(arrived):
    out = jnp.zeros((len(arrived),) + arrived[0][1].shape, arrived[0][1].dtype)
    for member, block in arrived:
        out = lax.dynamic_update_index_in_dim(out, block, member, 0)
    return out


def split_three(values):
    pieces = []
    for _ in range(3):
        piece = lax.reduce_precision(values, 8, 7)
        pieces.append(piece.astype(jnp.bfloat16))
        values = values - piece
    return pieces


def body(
    hidden,
    norm_gain,
    router,
    key_value_weight,
    query_master,
    output_master,
    key_value_cache,
    lengths,
    routes,
):
    steps, row_count, model_width = hidden.shape
    head_dim = key_value_weight.shape[1] // 2
    experts = router.shape[1]
    sections = lax.axis_size("section")
    heads = lax.axis_size("head")
    own_section = lax.axis_index("section")
    own_head = lax.axis_index("head")
    flat = steps * row_count
    depth = model_width // sections
    share = model_width // heads
    part = share // sections
    per_section = heads // sections
    outer = math.gcd(row_count, heads // 2)
    inner = heads // outer
    rows = row_count // outer
    own_outer = own_head // inner
    own_inner = own_head % inner
    own_flat = steps * rows
    core = 2 if sections == 4 else 1

    query_piece = query_master.astype(jnp.bfloat16)
    if core == 2:
        far = lax.ppermute(query_piece, "section", shift_pairs(sections, 2))
        near = jnp.concatenate([query_piece, far], axis=0)
        near_other = lax.ppermute(near, "section", shift_pairs(sections, 1))
        query_blocks = [
            (own_section, near[:depth]),
            (own_section ^ 2, near[depth:]),
            (own_section ^ 1, near_other[:depth]),
            (own_section ^ 3, near_other[depth:]),
        ]
    else:
        query_all = lax.all_gather(query_piece, "section", axis=0, tiled=True)
        query_blocks = [(i, query_all[i * depth : (i + 1) * depth]) for i in range(sections)]

    cache_rows = key_value_cache.reshape((outer, 1, rows) + key_value_cache.shape[1:])
    cache_rows = jnp.broadcast_to(
        cache_rows, (outer, inner, rows) + key_value_cache.shape[1:]
    ).reshape((heads, rows) + key_value_cache.shape[1:])
    cache_rows = lax.all_to_all(cache_rows, "head", 0, 0, tiled=True)
    cache_rows = cache_rows.transpose(1, 0, 2, 3).reshape(rows, -1, 2 * head_dim)

    output_piece = output_master.astype(jnp.bfloat16).reshape(per_section, sections, part, head_dim)
    if core == 2:
        halves = output_piece.reshape(per_section, 2, 2, part, head_dim)
        x_digit = own_section // 2
        c_digit = own_section % 2
        far = lax.ppermute(
            lax.dynamic_index_in_dim(halves, 1 - x_digit, 1, False),
            "section",
            shift_pairs(sections, 2),
        )
        both = in_order(
            [(x_digit, lax.dynamic_index_in_dim(halves, x_digit, 1, False)), (1 - x_digit, far)]
        )
        near_other = lax.ppermute(
            lax.dynamic_index_in_dim(both, 1 - c_digit, 2, False),
            "section",
            shift_pairs(sections, 1),
        )
        parts = in_order(
            [(c_digit, lax.dynamic_index_in_dim(both, c_digit, 2, False)), (1 - c_digit, near_other)]
        )
        parts = parts.transpose(1, 0, 2, 3, 4)
    else:
        parts = lax.all_to_all(output_piece.transpose(1, 0, 2, 3), "section", 0, 0, tiled=True)
    output_weight = lax.all_to_all(parts.reshape(heads, part, head_dim), "head", 0, 0, tiled=True)

    hidden_slice = lax.ppermute(
        lax.dynamic_slice_in_dim(hidden, own_head * share, share, 2),
        "section",
        [(i, (i + 1) % sections) for i in range(sections)],
    )

    mean_square = jnp.mean(hidden * hidden, axis=-1, keepdims=True)
    normed = (hidden * lax.rsqrt(mean_square + 1e-05) * norm_gain).astype(jnp.bfloat16)
    flat_rows = normed.reshape(flat, model_width)

    queries = 0.0
    for index, block in query_blocks:
        rows_block = lax.dynamic_slice_in_dim(flat_rows, index * depth, depth, 1)
        queries = queries + jnp.dot(rows_block, block, preferred_element_type=jnp.float32)
    queries = lax.reduce_precision(queries, 8, 7)

    slab = model_width // outer
    slab_rows = lax.dynamic_slice_in_dim(flat_rows, own_outer * slab, slab, 1)
    fresh_part = jnp.dot(
        slab_rows,
        lax.dynamic_slice_in_dim(key_value_weight, own_outer * slab, slab, 0),
        preferred_element_type=jnp.float32,
    )
    logit_part = jnp.dot(
        slab_rows,
        lax.dynamic_slice_in_dim(router, own_outer * slab, slab, 0),
        preferred_element_type=jnp.float32,
    )
    logit_part = jnp.pad(logit_part, ((0, 0), (0, -experts % head_dim)))
    message = jnp.concatenate([queries, fresh_part, logit_part], axis=1)
    message = message.reshape(steps, outer, rows, -1).transpose(1, 0, 2, 3)
    arrived = swap(lambda i: lax.dynamic_index_in_dim(message, i, 0, False), "head", inner, outer)
    summed = sum(block[..., head_dim:] for _, block in arrived)
    fresh_pairs = summed[..., : 2 * head_dim].astype(jnp.bfloat16)
    logits = summed[..., 2 * head_dim : 2 * head_dim + experts]
    queries = in_order([(member, block[..., :head_dim]) for member, block in arrived])
    queries = queries.astype(jnp.bfloat16)
    key_new = fresh_pairs[..., :head_dim]
    value_new = fresh_pairs[..., head_dim:]

    own_routes = lax.dynamic_slice_in_dim(routes, own_outer * rows, rows, 1)
    chosen = jnp.sum((own_routes[..., None] == jnp.arange(experts)).astype(jnp.float32), axis=2)
    picked = jax.nn.sigmoid(logits) * chosen
    gates = picked / jnp.sum(picked, axis=-1, keepdims=True)
    gates = lax.dynamic_index_in_dim(
        gates.reshape(steps, rows, outer, inner), own_inner, 3, False
    ).reshape(own_flat, outer)

    score_factor = 1.0 / math.sqrt(head_dim)
    step_order = jnp.arange(steps)
    fresh_mask = (step_order[None, :] <= step_order[:, None])[None, None]
    fresh_scores = (
        jnp.einsum("esrh,urh->resu", queries, key_new, preferred_element_type=jnp.float32)
        * score_factor
    )
    own_lengths = lax.dynamic_slice_in_dim(lengths, own_outer * rows, rows, 0)
    cache_mask = (jnp.arange(cache_rows.shape[1])[None, :] < own_lengths[:, None])[:, None, None, :]
    cache_scores = (
        jnp.einsum(
            "esrh,rph->resp",
            queries,
            cache_rows[..., :head_dim],
            preferred_element_type=jnp.float32,
        )
        * score_factor
    )
    highest = jnp.maximum(
        jnp.max(jnp.where(cache_mask, cache_scores, -jnp.inf), axis=-1, keepdims=True),
        jnp.max(jnp.where(fresh_mask, fresh_scores, -jnp.inf), axis=-1, keepdims=True),
    )
    cache_weights = jnp.where(cache_mask, jnp.exp(cache_scores - highest), 0.0)
    fresh_weights = jnp.where(fresh_mask, jnp.exp(fresh_scores - highest), 0.0)
    mixture = jnp.einsum(
        "resp,rph->resh",
        cache_weights,
        cache_rows[..., head_dim:],
        preferred_element_type=jnp.float32,
    ) + jnp.einsum("resu,urh->resh", fresh_weights, value_new, preferred_element_type=jnp.float32)
    denominator = jnp.sum(cache_weights, axis=-1, keepdims=True) + jnp.sum(
        fresh_weights, axis=-1, keepdims=True
    )
    attended = (mixture / denominator).astype(jnp.bfloat16)

    gate_pieces = jnp.concatenate(split_three(gates), axis=-1)
    gate_pieces = jnp.pad(gate_pieces, ((0, 0), (0, -gate_pieces.shape[1] % 128)))
    attended = attended.transpose(2, 0, 1, 3).reshape(own_flat, outer * head_dim)
    message = jnp.concatenate([attended, gate_pieces], axis=1)
    if core == 2:
        from_sections = swap(lambda i: message, "section", 1, sections)
        message = jnp.stack([block for _, block in from_sections])
    else:
        message = lax.all_to_all(
            jnp.broadcast_to(message[None], (sections,) + message.shape), "section", 0, 0, tiled=True
        )
    message = in_order(swap(lambda i: message, "head", 1, inner))
    message = in_order(swap(lambda i: message, "head", inner, outer))
    message = message.reshape(outer, inner, sections, steps, rows, -1)
    width = outer * head_dim
    vectors = message[..., :width].reshape(outer, inner, sections, steps, rows, outer, head_dim)
    vectors = vectors.transpose(2, 3, 0, 4, 5, 1, 6).reshape(sections * flat, experts, head_dim)
    pieces = message[..., width : width + 3 * outer].astype(jnp.float32)
    every_gate = (
        pieces[..., :outer] + pieces[..., outer : 2 * outer] + pieces[..., 2 * outer :]
    )
    every_gate = every_gate.transpose(2, 3, 0, 4, 5, 1).reshape(sections * flat, experts)

    per_expert = jnp.einsum(
        "neh,efh->nef", vectors, output_weight, preferred_element_type=jnp.float32
    )
    projected = jnp.sum(every_gate[..., None] * per_expert, axis=1).reshape(sections, flat, part)

    def group_of(member):
        return (member + sections - 1) % sections

    if core == 2:
        finished = in_order(
            swap(
                lambda i: lax.dynamic_index_in_dim(projected, group_of(i) ^ own_section, 0, False),
                "section",
                1,
                sections,
            )
        )
    else:
        finished = lax.all_to_all(
            jnp.roll(projected, 1, axis=0), "section", 0, 0, tiled=True
        )
    finished = finished.transpose(1, 0, 2).reshape(steps, row_count, share)
    return hidden_slice + finished


def solution(mesh):
    return jax.shard_map(
        body,
        mesh=mesh,
        in_specs=(
            P(None, "section", None),
            P(),
            P(),
            P(),
            P("section", "head"),
            P("section", "head"),
            P("section", "head", None),
            P("section"),
            P(None, "section", None),
        ),
        out_specs=P(None, "section", "head"),
        check_vma=False,
    )
```

time: 140 us -> 71 us (0.51)
  waiting for transfers between devices: 87.1 us -> 22.1 us
  starting transfers between devices: 5.79 us -> 29.2 us
  blocking collectives: 18.6 us -> 0 us
  between operations: 13.3 us -> 0.76 us
  local copies, waits for them, and re-layouts: 0.87 us -> 8.62 us
  matrix products: 9.74 us -> 3.52 us
  other arithmetic: 3.71 us -> 6.32 us
    all_gather x3 -> x0, waiting for transfers between devices: 82.2 us -> none  [the longest x1 47.6 us: body(): gathered = lax.all_gather(key_value_cache, 'head', axis=1, tiled=True)]
    ppermute x1 -> x18, starting transfers between devices: 0.06 us -> 19.9 us  [the longest x13 14.7 us: swap(): lax.ppermute(pick(other), axis, shift_pairs(count, offset, stride, size))]
    all_gather x1 -> x0, blocking collectives: 18.6 us -> none  [body(): lax.all_gather(attended[:, :, None, :], 'head', axis=2, tiled=True)]
    ppermute x1 -> x18, waiting for transfers between devices: 4.2 us -> 22.1 us  [the longest x13 20.1 us: swap(): lax.ppermute(pick(other), axis, shift_pairs(count, offset, stride, size))]
    dot_general x8 -> x11, matrix products: 9.74 us -> 3.52 us  [the longest x1 1.43 us: body(): jnp.dot(slab_rows, lax.dynamic_slice_in_dim(key_value_weight, own_outer *...]
    all_to_all x1 -> x2, starting transfers between devices: 5.65 us -> 9.31 us  [the longest x1 5.83 us: body(): cache_rows = lax.all_to_all(cache_rows, 'head', 0, 0, tiled=True)]
    dynamic_update_slice x0 -> x18, local copies, waits for them, and re-layouts: none -> 2.53 us  [in_order(): out = lax.dynamic_update_index_in_dim(out, block, member, 0)]
    broadcast_in_dim x0 -> x8, local copies, waits for them, and re-layouts: none -> 1.83 us  [the longest x1 1.63 us: body(): jnp.broadcast_to(cache_rows, (outer, inner, rows) + key_value_cache.shape...]
  transfers between devices with their start and end apart: 5 -> 20, of which waited for: 4 -> 8; matrix products, arithmetic and copies ran while one was open for 8% -> 22% of each run, Pallas kernels for 0% -> 0%
where the time goes in v1:
time: 71 us; the launch traced here: 70.6 us
  starting transfers between devices  29.2 us (41%)
  waiting for transfers between devices  22.1 us (31%)
  local copies, waits for them, and re-layouts  8.62 us (12%)
  other arithmetic  6.32 us (9%)
  matrix products  3.52 us (5%)
  between operations  0.76 us (1%)
    ppermute x13, waiting for transfers between devices, swap(): lax.ppermute(pick(other), axis, shift_pairs(count, offset, stride, size))  20.1 us
    ppermute x13, starting transfers between devices, swap(): lax.ppermute(pick(other), axis, shift_pairs(count, offset, stride, size))  14.7 us
    all_to_all x1, starting transfers between devices, body(): cache_rows = lax.all_to_all(cache_rows, 'head', 0, 0, tiled=True)  5.83 us
    all_to_all x1, starting transfers between devices, body(): lax.all_to_all(parts.reshape(heads, part, head_dim), 'head', 0, 0, tiled=...  3.47 us
    ppermute x1, starting transfers between devices, body(): far = lax.ppermute(query_piece, 'section', shift_pairs(sections, 2))  3.04 us
    dynamic_update_slice x18, local copies, waits for them, and re-layouts, in_order(): out = lax.dynamic_update_index_in_dim(out, block, member, 0)  2.53 us
    ppermute x1, waiting for transfers between devices, body(): lax.ppermute(lax.dynamic_index_in_dim(halves, 1 - x_digit, 1, False), 'se...  2.07 us
    broadcast_in_dim x1, local copies, waits for them, and re-layouts, body(): jnp.broadcast_to(cache_rows, (outer, inner, rows) + key_value_cache.shape...  1.63 us
  transfers between devices with their start and end apart: 20, of which 8 were waited for; matrix products, arithmetic and copies ran while one was open for 22% of the time, Pallas kernels for 0%

profile of v1, /device:TPU:0, one launch (start us, length us, event | category | flops | bytes accessed | tf_op | source)
XLA Modules:
  0.0 70.6 jit_solution(1313482465201724317)
XLA Ops:
  0.0 1.3 %convert_element_type.37 = bf16[1792,128]{1,0:T(8,128)(2,1)S(1)} convert(f32[1792,128]{1,0:T(8,128)} %param.13) | non-fusion elementwise | flops 229376 | bytes 1376256 | tf_op jit(solution)/shard_map/convert_element_type | solution.py:83
  1.3 3.0 %collective-permute-start.1 = (bf16[1792,128]{1,0:T(8,128)(2,1)S(1)}, bf16[1792,128]{1,0:T(8,128)(2,1)S(1)}, u32[]{:S(2)}, u32[]{:S(2)}) collective-permute-start(bf16[1792,128]{1,0:T(8,128)(2,1)S(1)} %convert_element_type.37), channel_id=1, source_target_pairs={{0,16},{8,24},{16,0},{24,8},{1,17},{9,25},{17,1},{25,9},{2,18},{10... | collective-permute-start | bytes 1376264 | tf_op jit(solution)/shard_map/ppermute | solution.py:85
  4.4 1.6 %broadcast_in_dim.139 = bf16[4,2,2,32,256]{4,3,2,1,0:T(8,128)(2,1)} broadcast(bf16[4,2,32,256]{3,2,1,0:T(8,128)(2,1)} %bitcast.156), dimensions={0,2,3,4} | broadcast | bytes 393216 | tf_op jit(solution)/shard_map/broadcast_in_dim | solution.py:99
  6.0 5.8 %all-to-all-start = ((bf16[8,2,32,256]{3,2,1,0:T(8,128)(2,1)}), bf16[8,2,32,256]{3,2,1,0:T(8,128)(2,1)S(1)}, u32[]{:S(2)}, u32[]{:S(2)}) async-start(bf16[8,2,32,256]{3,2,1,0:T(8,128)(2,1)} %bitcast.14), calls=%async_computation | async-start | bytes 524288 | tf_op jit(solution)/shard_map/all_to_all | solution.py:102
  11.8 1.2 %convert_element_type.45 = bf16[1792,128]{1,0:T(8,128)(2,1)S(1)} convert(f32[1792,128]{1,0:T(8,128)} %param.14) | non-fusion elementwise | flops 229376 | bytes 1376256 | tf_op jit(solution)/shard_map/convert_element_type | solution.py:105
  13.1 0.7 dynamic-slice_bitcast_fusion
  13.8 0.5 collective-permute-start.13
  14.4 0.2 multiply_reduce_fusion
  14.7 0.2 fusion.9
  14.9 1.4 %fusion.7 = f32[32,256]{1,0:T(8,128)S(1)} fusion(bf16[7168,256]{1,0:T(8,128)(2,1)} %param.12, s32[]{:T(128)S(6)} %select_n.172, bf16[32,7168]{1,0:T(8,128)(2,1)S(1)} %fusion.9), kind=kOutput, calls=%fused_computation.14 | convolution fusion | flops 29360128 | bytes 1065984 | tf_op jit(solution)/shard_map/dot_general | solution.py:149
  16.3 0.2 fusion.20
  16.7 0.1 copy.85
  16.8 0.1 convert_reduce_fusion
  17.2 0.2 fusion.18
  17.4 1.0 %pad_maximum_fusion = bf16[3584,128]{1,0:T(8,128)(2,1)} fusion(bf16[1792,128]{1,0:T(8,128)(2,1)S(1)} %collective-permute-done.1, bf16[1792,128]{1,0:T(8,128)(2,1)S(1)} %convert_element_type.37), kind=kLoop, calls=%fused_computation.13 | loop fusion | flops 1835008 | bytes 1835008 | tf_op jit(solution)/shard_map/concatenate | solution.py:86
  18.4 1.6 %collective-permute-start.2 = (bf16[3584,128]{1,0:T(8,128)(2,1)}, bf16[3584,128]{1,0:T(8,128)(2,1)S(1)}, u32[]{:S(2)}, u32[]{:S(2)}) collective-permute-start(bf16[3584,128]{1,0:T(8,128)(2,1)} %pad_maximum_fusion), channel_id=1, source_target_pairs={{0,8},{8,0},{16,24},{24,16},{1,9},{9,1},{17,25},{25,17},{2,10},{10... | collective-permute-start | bytes 2752520 | tf_op jit(solution)/shard_map/ppermute | solution.py:87
  19.9 2.1 %collective-permute-done.13 = bf16[2,2,224,128]{3,2,1,0:T(8,128)(2,1)S(1)} collective-permute-done((bf16[2,2,224,128]{3,2,1,0:T(8,128)(2,1)}, bf16[2,2,224,128]{3,2,1,0:T(8,128)(2,1)S(1)}, u32[]{:S(2)}, u32[]{:S(2)}) %collective-permute-start.13) | collective-permute-done | bytes 229408 | tf_op jit(solution)/shard_map/ppermute | solution.py:110
  22.2 0.8 %broadcast.53 = bf16[2,2,2,224,128]{4,3,2,0,1:T(8,128)(2,1)} broadcast(bf16[]{:T(256)} %constant.209.clone.1), dimensions={} | broadcast | bytes 458754 | tf_op jit(solution)/shard_map/broadcast.3
  23.0 0.7 %bitcast_dynamic-update-slice_fusion.1 = bf16[2,2,2,224,128]{4,3,2,0,1:T(8,128)(2,1)} fusion(bf16[2,2,2,224,128]{4,3,2,0,1:T(8,128)(2,1)} %broadcast.53, s32[]{:T(128)S(6)} %select_n.189, bf16[2,2,1,224,128]{4,3,2,0,1:T(8,128)(2,1)S(1)} %get-tuple-element.10), kind=kLoop, calls=%fused_computation.23 | loop fusion | bytes 458756 | tf_op jit(solution)/shard_map/jit(dynamic_update_index_in_dim)/dynamic_update_slice | solution.py:39
  23.8 0.2 convolution_add_fusion.2
  24.0 0.2 fusion.10
  24.2 0.2 fusion.5
  24.6 1.8 %collective-permute-start.3 = (f32[4,2,512]{2,0,1:T(4,128)S(1)}, f32[4,2,512]{2,0,1:T(4,128)S(1)}, u32[]{:S(2)}, u32[]{:S(2)}) collective-permute-start(f32[4,2,512]{2,0,1:T(4,128)S(1)} %bitcast.163), channel_id=1, source_target_pairs={{0,2},{1,3},{2,0},{3,1},{4,6},{5,7},{6,4},{7,5},{8,10},{9,11},{10,... | collective-permute-start | bytes 49160 | tf_op jit(solution)/shard_map/ppermute | solution.py:31
  26.4 2.4 %collective-permute-start.4 = (f32[4,2,512]{2,0,1:T(4,128)S(1)}, f32[4,2,512]{2,0,1:T(4,128)S(1)}, u32[]{:S(2)}, u32[]{:S(2)}) collective-permute-start(f32[4,2,512]{2,0,1:T(4,128)S(1)} %bitcast.164), channel_id=1, source_target_pairs={{0,4},{1,5},{2,6},{3,7},{4,0},{5,1},{6,2},{7,3},{8,12},{9,13},{10,... | collective-permute-start | bytes 49160 | tf_op jit(solution)/shard_map/ppermute | solution.py:31
  28.7 0.3 collective-permute-start.5
  29.1 1.9 %collective-permute-done.4 = f32[4,2,512]{2,0,1:T(4,128)S(1)} collective-permute-done((f32[4,2,512]{2,0,1:T(4,128)S(1)}, f32[4,2,512]{2,0,1:T(4,128)S(1)}, u32[]{:S(2)}, u32[]{:S(2)}) %collective-permute-start.4) | collective-permute-done | bytes 16416 | tf_op jit(solution)/shard_map/ppermute | solution.py:31
  31.0 3.3 %collective-permute-done.5 = f32[4,2,512]{2,0,1:T(4,128)S(1)} collective-permute-done((f32[4,2,512]{2,0,1:T(4,128)S(1)}, f32[4,2,512]{2,0,1:T(4,128)S(1)}, u32[]{:S(2)}, u32[]{:S(2)}) %collective-permute-start.5) | collective-permute-done | bytes 16416 | tf_op jit(solution)/shard_map/ppermute | solution.py:31
  34.3 0.2 select_reduce_fusion.1
  34.5 0.2 select_reduce_fusion
  34.8 0.2 fusion.24
  34.9 0.2 fusion.14
  35.2 0.1 fusion.54
  35.4 0.1 copy.87
  35.5 0.1 copy.88
  35.6 0.2 fusion.6
  35.9 0.9 %collective-permute-start.7 = (bf16[8,640]{1,0:T(8,128)(2,1)S(1)}, bf16[8,640]{1,0:T(8,128)(2,1)S(1)}, u32[]{:S(2)}, u32[]{:S(2)}) collective-permute-start(bf16[8,640]{1,0:T(8,128)(2,1)S(1)} %get-tuple-element.22), channel_id=1, source_target_pairs={{0,16},{8,24},{16,0},{24,8},{1,17},{9,25},{17,1},{25,9},{2,18},{10... | collective-permute-start | bytes 30728 | tf_op jit(solution)/shard_map/ppermute | solution.py:31
  36.8 1.0 %collective-permute-start.8 = (bf16[8,640]{1,0:T(8,128)(2,1)S(1)}, bf16[8,640]{1,0:T(8,128)(2,1)S(1)}, u32[]{:S(2)}, u32[]{:S(2)}) collective-permute-start(bf16[8,640]{1,0:T(8,128)(2,1)S(1)} %get-tuple-element.22), channel_id=1, source_target_pairs={{0,24},{8,16},{16,8},{24,0},{1,25},{9,17},{17,9},{25,1},{2,26},{10... | collective-permute-start | bytes 30728 | tf_op jit(solution)/shard_map/ppermute | solution.py:31
  37.8 0.7 %bitcast_dynamic-update-slice_fusion = bf16[2,2,2,224,128]{4,3,2,0,1:T(8,128)(2,1)} fusion(bf16[2,2,2,224,128]{4,3,2,0,1:T(8,128)(2,1)} %bitcast_dynamic-update-slice_fusion.1, s32[]{:T(128)S(6)} %select_n.190, bf16[2,2,224,128]{3,2,1,0:T(8,128)(2,1)S(1)} %collective-permute-done.14), kind=kLoop, calls=%fused_computation.22 | loop fusion | bytes 458756 | tf_op jit(solution)/shard_map/jit(dynamic_update_index_in_dim)/dynamic_update_slice | solution.py:39
  38.5 3.5 %all-to-all-start.1 = ((bf16[8,224,128]{2,1,0:T(8,128)(2,1)}), bf16[8,224,128]{2,1,0:T(8,128)(2,1)S(1)}, u32[]{:S(2)}, u32[]{:S(2)}) async-start(bf16[8,224,128]{2,1,0:T(8,128)(2,1)} %bitcast.49), calls=%async_computation.1 | async-start | bytes 917504 | tf_op jit(solution)/shard_map/all_to_all | solution.py:129
  42.0 2.0 %collective-permute-start.9 = (bf16[4,8,640]{2,1,0:T(8,128)(2,1)S(1)}, bf16[4,8,640]{2,1,0:T(8,128)(2,1)S(1)}, u32[]{:S(2)}, u32[]{:S(2)}) collective-permute-start(bf16[4,8,640]{2,1,0:T(8,128)(2,1)S(1)} %get-tuple-element.19), channel_id=1, source_target_pairs={{0,1},{1,0},{2,3},{3,2},{4,5},{5,4},{6,7},{7,6},{8,9},{9,8},{10,11... | collective-permute-start | bytes 122888 | tf_op jit(solution)/shard_map/ppermute | solution.py:31
  44.1 4.5 %collective-permute-done.9 = bf16[4,8,640]{2,1,0:T(8,128)(2,1)S(1)} collective-permute-done((bf16[4,8,640]{2,1,0:T(8,128)(2,1)S(1)}, bf16[4,8,640]{2,1,0:T(8,128)(2,1)S(1)}, u32[]{:S(2)}, u32[]{:S(2)}) %collective-permute-start.9) | collective-permute-done | bytes 40992 | tf_op jit(solution)/shard_map/ppermute | solution.py:31
  48.6 1.1 %collective-permute-start.10 = (bf16[2,4,8,640]{3,1,2,0:T(4,128)(2,1)S(1)}, bf16[2,4,8,640]{3,1,2,0:T(4,128)(2,1)S(1)}, u32[]{:S(2)}, u32[]{:S(2)}) collective-permute-start(bf16[2,4,8,640]{3,1,2,0:T(4,128)(2,1)S(1)} %copy_dynamic-update-slice_fusion), channel_id=1, source_target_pairs={{0,2},{1,3},{2,0},{3,1},{4,6},{5,7},{6,4},{7,5},{8,10},{9,11},{10,... | collective-permute-start | bytes 245768 | tf_op jit(solution)/shard_map/ppermute | solution.py:31
  49.6 2.3 %collective-permute-start.11 = (bf16[2,4,8,640]{3,1,2,0:T(4,128)(2,1)S(1)}, bf16[2,4,8,640]{3,1,2,0:T(4,128)(2,1)S(1)}, u32[]{:S(2)}, u32[]{:S(2)}) collective-permute-start(bf16[2,4,8,640]{3,1,2,0:T(4,128)(2,1)S(1)} %copy_dynamic-update-slice_fusion), channel_id=1, source_target_pairs={{0,4},{1,5},{2,6},{3,7},{4,0},{5,1},{6,2},{7,3},{8,12},{9,13},{10,... | collective-permute-start | bytes 245768 | tf_op jit(solution)/shard_map/ppermute | solution.py:31
  51.9 1.1 %collective-permute-start.12 = (bf16[2,4,8,640]{3,1,2,0:T(4,128)(2,1)S(1)}, bf16[2,4,8,640]{3,1,2,0:T(4,128)(2,1)S(1)}, u32[]{:S(2)}, u32[]{:S(2)}) collective-permute-start(bf16[2,4,8,640]{3,1,2,0:T(4,128)(2,1)S(1)} %copy_dynamic-update-slice_fusion), channel_id=1, source_target_pairs={{0,6},{1,7},{2,4},{3,5},{4,2},{5,3},{6,0},{7,1},{8,14},{9,15},{10,... | collective-permute-start | bytes 245768 | tf_op jit(solution)/shard_map/ppermute | solution.py:31
  53.1 0.2 collective-permute-done.10
  53.4 8.2 %collective-permute-done.11 = bf16[2,4,8,640]{3,1,2,0:T(4,128)(2,1)S(1)} collective-permute-done((bf16[2,4,8,640]{3,1,2,0:T(4,128)(2,1)S(1)}, bf16[2,4,8,640]{3,1,2,0:T(4,128)(2,1)S(1)}, u32[]{:S(2)}, u32[]{:S(2)}) %collective-permute-start.11) | collective-permute-done | bytes 81952 | tf_op jit(solution)/shard_map/ppermute | solution.py:31
  61.8 0.1 slice.103
  61.9 0.1 reshape.122
  62.0 0.2 copy.95
  62.2 0.2 fusion.13
  62.4 1.0 %copy.91 = f32[4,4,4,2,4,2]{3,2,1,0,5,4:T(4,128)S(1)} copy(f32[4,4,4,2,4,2]{4,0,3,1,5,2:T(4,128)S(1)} %fusion.13) | data formatting | bytes 8192 | tf_op jit(solution)/shard_map/transpose | solution.py:235
  63.5 0.3 mul.85
  63.7 0.3 fusion.1
  64.0 0.1 copy.96
  64.2 0.9 %collective-permute-start.16 = (f32[32,224]{1,0:T(8,128)S(1)}, f32[32,224]{1,0:T(8,128)S(1)}, u32[]{:S(2)}, u32[]{:S(2)}) collective-permute-start(f32[32,224]{1,0:T(8,128)S(1)} %get-tuple-element.12), channel_id=1, source_target_pairs={{0,16},{8,24},{16,0},{24,8},{1,17},{9,25},{17,1},{25,9},{2,18},{10... | collective-permute-start | bytes 86024 | tf_op jit(solution)/shard_map/ppermute | solution.py:31
  65.1 1.0 %collective-permute-start.17 = (f32[32,224]{1,0:T(8,128)S(1)}, f32[32,224]{1,0:T(8,128)S(1)}, u32[]{:S(2)}, u32[]{:S(2)}) collective-permute-start(f32[32,224]{1,0:T(8,128)S(1)} %get-tuple-element.11), channel_id=1, source_target_pairs={{0,24},{8,16},{16,8},{24,0},{1,25},{9,17},{17,9},{25,1},{2,26},{10... | collective-permute-start | bytes 86024 | tf_op jit(solution)/shard_map/ppermute | solution.py:31
  66.1 0.2 dynamic_update_slice.73
  66.4 0.2 dynamic_update_slice.74
  66.6 1.8 %collective-permute-done.16 = f32[32,224]{1,0:T(8,128)S(1)} collective-permute-done((f32[32,224]{1,0:T(8,128)S(1)}, f32[32,224]{1,0:T(8,128)S(1)}, u32[]{:S(2)}, u32[]{:S(2)}) %collective-permute-start.16) | collective-permute-done | bytes 28704 | tf_op jit(solution)/shard_map/ppermute | solution.py:31
  68.3 0.2 dynamic_update_slice.75
  68.5 0.2 collective-permute-done.17
  68.7 0.2 dynamic_update_slice.76
  68.9 0.1 reshape.117
  69.0 1.6 %add.262 = f32[4,8,896]{2,1,0:T(8,128)} add(f32[4,8,896]{2,1,0:T(8,128)} %collective-permute-done, f32[4,8,896]{2,1,0:T(8,128)S(1)} %reshape.117) | non-fusion elementwise | flops 28672 | bytes 344064 | tf_op jit(solution)/shard_map/add | solution.py:259
  (77 shorter events, 1.7 us)
Async XLA Ops:
  0.0 16.3 %copy-start = (bf16[7168,8]{0,1:T(8,128)(2,1)S(1)}, bf16[7168,8]{0,1:T(8,128)(2,1)}, u32[]{:S(2)}) copy-start(bf16[7168,8]{0,1:T(8,128)(2,1)} %param.11) | copy-start | bytes 344068
  0.0 14.3 %copy-start.1 = (f32[4,8,7168]{2,1,0:T(8,128)S(1)}, f32[4,8,7168]{2,1,0:T(8,128)}, u32[]{:S(2)}) copy-start(f32[4,8,7168]{2,1,0:T(8,128)} %param.9) | copy-start | bytes 2752516
  0.0 14.7 %copy-start.2 = (f32[7168]{0:T(1024)S(1)}, f32[7168]{0:T(1024)}, u32[]{:S(2)}) copy-start(f32[7168]{0:T(1024)} %param.10) | copy-start | bytes 86020
  1.3 15.2 %copy-start.4 = (s32[8]{0:T(128)S(1)}, s32[8]{0:T(128)}, u32[]{:S(2)}) copy-start(s32[8]{0:T(128)} %param.16) | copy-start | bytes 100
  1.3 15.3 %copy-start.3 = (s32[4,8,4]{1,2,0:T(4,128)S(1)}, s32[4,8,4]{1,2,0:T(4,128)}, u32[]{:S(2)}) copy-start(s32[4,8,4]{1,2,0:T(4,128)} %param.17) | copy-start | bytes 1540
  1.3 16.0 %collective-permute-start.1 = (bf16[1792,128]{1,0:T(8,128)(2,1)S(1)}, bf16[1792,128]{1,0:T(8,128)(2,1)S(1)}, u32[]{:S(2)}, u32[]{:S(2)}) collective-permute-start(bf16[1792,128]{1,0:T(8,128)(2,1)S(1)} %convert_element_type.37), channel_id=1, source_target_pairs={{0,16},{8,24},{16,0},{24,8},{1,17},{9,25},{17,1},{25,9},{2,18},{10... | collective-permute-start | bytes 1376264 | tf_op jit(solution)/shard_map/ppermute | solution.py:85
  6.0 17.8 %all-to-all-start = ((bf16[8,2,32,256]{3,2,1,0:T(8,128)(2,1)}), bf16[8,2,32,256]{3,2,1,0:T(8,128)(2,1)S(1)}, u32[]{:S(2)}, u32[]{:S(2)}) async-start(bf16[8,2,32,256]{3,2,1,0:T(8,128)(2,1)} %bitcast.14), calls=%async_computation | async-start | bytes 524288 | tf_op jit(solution)/shard_map/all_to_all | solution.py:102
  13.8 8.2 %collective-permute-start.13 = (bf16[2,2,224,128]{3,2,1,0:T(8,128)(2,1)}, bf16[2,2,224,128]{3,2,1,0:T(8,128)(2,1)S(1)}, u32[]{:S(2)}, u32[]{:S(2)}) collective-permute-start(bf16[2,2,224,128]{3,2,1,0:T(8,128)(2,1)} %dynamic-slice_bitcast_fusion), channel_id=1, source_target_pairs={{0,16},{8,24},{16,0},{24,8},{1,17},{9,25},{17,1},{25,9},{2,18},{10... | collective-permute-start | bytes 688136 | tf_op jit(solution)/shard_map/ppermute | solution.py:110
  14.3 54.7 %collective-permute-start = (f32[4,8,896]{2,1,0:T(8,128)S(1)}, f32[4,8,896]{2,1,0:T(8,128)}, u32[]{:S(2)}, u32[]{:S(2)}) collective-permute-start(f32[4,8,896]{2,1,0:T(8,128)S(1)} %constant_dynamic-slice_fusion.9), channel_id=1, source_target_pairs={{0,8},{8,16},{16,24},{24,0},{1,9},{9,17},{17,25},{25,1},{2,10},{10... | collective-permute-start | bytes 344072 | tf_op jit(solution)/shard_map/ppermute | solution.py:131
  18.4 5.7 %collective-permute-start.2 = (bf16[3584,128]{1,0:T(8,128)(2,1)}, bf16[3584,128]{1,0:T(8,128)(2,1)S(1)}, u32[]{:S(2)}, u32[]{:S(2)}) collective-permute-start(bf16[3584,128]{1,0:T(8,128)(2,1)} %pad_maximum_fusion), channel_id=1, source_target_pairs={{0,8},{8,0},{16,24},{24,16},{1,9},{9,1},{17,25},{25,17},{2,10},{10... | collective-permute-start | bytes 2752520 | tf_op jit(solution)/shard_map/ppermute | solution.py:87
  22.1 15.6 %collective-permute-start.14 = (bf16[2,2,224,128]{3,2,1,0:T(8,128)(2,1)S(1)}, bf16[2,2,224,128]{3,2,1,0:T(8,128)(2,1)S(1)}, u32[]{:S(2)}, u32[]{:S(2)}) collective-permute-start(bf16[2,2,224,128]{3,2,1,0:T(8,128)(2,1)S(1)} %bitcast.155), channel_id=1, source_target_pairs={{0,8},{8,0},{16,24},{24,16},{1,9},{9,1},{17,25},{25,17},{2,10},{10... | collective-permute-start | bytes 688136 | tf_op jit(solution)/shard_map/ppermute | solution.py:118
  24.6 4.5 %collective-permute-start.3 = (f32[4,2,512]{2,0,1:T(4,128)S(1)}, f32[4,2,512]{2,0,1:T(4,128)S(1)}, u32[]{:S(2)}, u32[]{:S(2)}) collective-permute-start(f32[4,2,512]{2,0,1:T(4,128)S(1)} %bitcast.163), channel_id=1, source_target_pairs={{0,2},{1,3},{2,0},{3,1},{4,6},{5,7},{6,4},{7,5},{8,10},{9,11},{10,... | collective-permute-start | bytes 49160 | tf_op jit(solution)/shard_map/ppermute | solution.py:31
  26.4 4.6 %collective-permute-start.4 = (f32[4,2,512]{2,0,1:T(4,128)S(1)}, f32[4,2,512]{2,0,1:T(4,128)S(1)}, u32[]{:S(2)}, u32[]{:S(2)}) collective-permute-start(f32[4,2,512]{2,0,1:T(4,128)S(1)} %bitcast.164), channel_id=1, source_target_pairs={{0,4},{1,5},{2,6},{3,7},{4,0},{5,1},{6,2},{7,3},{8,12},{9,13},{10,... | collective-permute-start | bytes 49160 | tf_op jit(solution)/shard_map/ppermute | solution.py:31
  28.7 5.5 %collective-permute-start.5 = (f32[4,2,512]{2,0,1:T(4,128)S(1)}, f32[4,2,512]{2,0,1:T(4,128)S(1)}, u32[]{:S(2)}, u32[]{:S(2)}) collective-permute-start(f32[4,2,512]{2,0,1:T(4,128)S(1)} %bitcast.165), channel_id=1, source_target_pairs={{0,6},{1,7},{2,4},{3,5},{4,2},{5,3},{6,0},{7,1},{8,14},{9,15},{10,... | collective-permute-start | bytes 49160 | tf_op jit(solution)/shard_map/ppermute | solution.py:31
  35.9 6.1 %collective-permute-start.6 = (bf16[8,640]{1,0:T(8,128)(2,1)S(1)}, bf16[8,640]{1,0:T(8,128)(2,1)S(1)}, u32[]{:S(2)}, u32[]{:S(2)}) collective-permute-start(bf16[8,640]{1,0:T(8,128)(2,1)S(1)} %get-tuple-element.22), channel_id=1, source_target_pairs={{0,8},{8,0},{16,24},{24,16},{1,9},{9,1},{17,25},{25,17},{2,10},{10... | collective-permute-start | bytes 30728 | tf_op jit(solution)/shard_map/ppermute | solution.py:31
  35.9 6.1 %collective-permute-start.7 = (bf16[8,640]{1,0:T(8,128)(2,1)S(1)}, bf16[8,640]{1,0:T(8,128)(2,1)S(1)}, u32[]{:S(2)}, u32[]{:S(2)}) collective-permute-start(bf16[8,640]{1,0:T(8,128)(2,1)S(1)} %get-tuple-element.22), channel_id=1, source_target_pairs={{0,16},{8,24},{16,0},{24,8},{1,17},{9,25},{17,1},{25,9},{2,18},{10... | collective-permute-start | bytes 30728 | tf_op jit(solution)/shard_map/ppermute | solution.py:31
  36.8 5.2 %collective-permute-start.8 = (bf16[8,640]{1,0:T(8,128)(2,1)S(1)}, bf16[8,640]{1,0:T(8,128)(2,1)S(1)}, u32[]{:S(2)}, u32[]{:S(2)}) collective-permute-start(bf16[8,640]{1,0:T(8,128)(2,1)S(1)} %get-tuple-element.22), channel_id=1, source_target_pairs={{0,24},{8,16},{16,8},{24,0},{1,25},{9,17},{17,9},{25,1},{2,26},{10... | collective-permute-start | bytes 30728 | tf_op jit(solution)/shard_map/ppermute | solution.py:31
  38.5 25.2 %all-to-all-start.1 = ((bf16[8,224,128]{2,1,0:T(8,128)(2,1)}), bf16[8,224,128]{2,1,0:T(8,128)(2,1)S(1)}, u32[]{:S(2)}, u32[]{:S(2)}) async-start(bf16[8,224,128]{2,1,0:T(8,128)(2,1)} %bitcast.49), calls=%async_computation.1 | async-start | bytes 917504 | tf_op jit(solution)/shard_map/all_to_all | solution.py:129
  42.0 6.5 %collective-permute-start.9 = (bf16[4,8,640]{2,1,0:T(8,128)(2,1)S(1)}, bf16[4,8,640]{2,1,0:T(8,128)(2,1)S(1)}, u32[]{:S(2)}, u32[]{:S(2)}) collective-permute-start(bf16[4,8,640]{2,1,0:T(8,128)(2,1)S(1)} %get-tuple-element.19), channel_id=1, source_target_pairs={{0,1},{1,0},{2,3},{3,2},{4,5},{5,4},{6,7},{7,6},{8,9},{9,8},{10,11... | collective-permute-start | bytes 122888 | tf_op jit(solution)/shard_map/ppermute | solution.py:31
  48.6 4.8 %collective-permute-start.10 = (bf16[2,4,8,640]{3,1,2,0:T(4,128)(2,1)S(1)}, bf16[2,4,8,640]{3,1,2,0:T(4,128)(2,1)S(1)}, u32[]{:S(2)}, u32[]{:S(2)}) collective-permute-start(bf16[2,4,8,640]{3,1,2,0:T(4,128)(2,1)S(1)} %copy_dynamic-update-slice_fusion), channel_id=1, source_target_pairs={{0,2},{1,3},{2,0},{3,1},{4,6},{5,7},{6,4},{7,5},{8,10},{9,11},{10,... | collective-permute-start | bytes 245768 | tf_op jit(solution)/shard_map/ppermute | solution.py:31
  49.6 12.0 %collective-permute-start.11 = (bf16[2,4,8,640]{3,1,2,0:T(4,128)(2,1)S(1)}, bf16[2,4,8,640]{3,1,2,0:T(4,128)(2,1)S(1)}, u32[]{:S(2)}, u32[]{:S(2)}) collective-permute-start(bf16[2,4,8,640]{3,1,2,0:T(4,128)(2,1)S(1)} %copy_dynamic-update-slice_fusion), channel_id=1, source_target_pairs={{0,4},{1,5},{2,6},{3,7},{4,0},{5,1},{6,2},{7,3},{8,12},{9,13},{10,... | collective-permute-start | bytes 245768 | tf_op jit(solution)/shard_map/ppermute | solution.py:31
  51.9 9.8 %collective-permute-start.12 = (bf16[2,4,8,640]{3,1,2,0:T(4,128)(2,1)S(1)}, bf16[2,4,8,640]{3,1,2,0:T(4,128)(2,1)S(1)}, u32[]{:S(2)}, u32[]{:S(2)}) collective-permute-start(bf16[2,4,8,640]{3,1,2,0:T(4,128)(2,1)S(1)} %copy_dynamic-update-slice_fusion), channel_id=1, source_target_pairs={{0,6},{1,7},{2,4},{3,5},{4,2},{5,3},{6,0},{7,1},{8,14},{9,15},{10,... | collective-permute-start | bytes 245768 | tf_op jit(solution)/shard_map/ppermute | solution.py:31
  64.2 2.2 %collective-permute-start.15 = (f32[32,224]{1,0:T(8,128)S(1)}, f32[32,224]{1,0:T(8,128)S(1)}, u32[]{:S(2)}, u32[]{:S(2)}) collective-permute-start(f32[32,224]{1,0:T(8,128)S(1)} %get-tuple-element.13), channel_id=1, source_target_pairs={{0,8},{8,0},{16,24},{24,16},{1,9},{9,1},{17,25},{25,17},{2,10},{10... | collective-permute-start | bytes 86024 | tf_op jit(solution)/shard_map/ppermute | solution.py:31
  64.2 4.1 %collective-permute-start.16 = (f32[32,224]{1,0:T(8,128)S(1)}, f32[32,224]{1,0:T(8,128)S(1)}, u32[]{:S(2)}, u32[]{:S(2)}) collective-permute-start(f32[32,224]{1,0:T(8,128)S(1)} %get-tuple-element.12), channel_id=1, source_target_pairs={{0,16},{8,24},{16,0},{24,8},{1,17},{9,25},{17,1},{25,9},{2,18},{10... | collective-permute-start | bytes 86024 | tf_op jit(solution)/shard_map/ppermute | solution.py:31
  65.1 3.6 %collective-permute-start.17 = (f32[32,224]{1,0:T(8,128)S(1)}, f32[32,224]{1,0:T(8,128)S(1)}, u32[]{:S(2)}, u32[]{:S(2)}) collective-permute-start(f32[32,224]{1,0:T(8,128)S(1)} %get-tuple-element.11), channel_id=1, source_target_pairs={{0,24},{8,16},{16,8},{24,0},{1,25},{9,17},{17,9},{25,1},{2,26},{10... | collective-permute-start | bytes 86024 | tf_op jit(solution)/shard_map/ppermute | solution.py:31
